TPU v7x, 256 devices: a whole 4x4x8 slice. The times are simulated.
256 devices in a mesh: row: 16 (over z, core), col: 16 (over y, x).
Axes of the slice: x: 4, y: 4, z: 8, core: 2. Of those that a mesh axis runs over, the one named last changes fastest.
Arguments:
- y_panels: bfloat16 [2, 1024, 4096], P(None, 'row', 'col'), may hold values from -6 to 6
- tri_inverse: bfloat16 [2, 1024, 1024], P(None, 'row', 'col'), may hold values from -1.5 to 1.5, as said below
- coupling: bfloat16 [1024, 1024], P('row', 'col'), may hold values from -0.1875 to 0.1875
- rest_factor: bfloat16 [40960, 2, 1024], P('row'), may hold values from -0.03125 to 0.03125
- rest_coeffs: bfloat16 [40960, 4096], P('row', 'col'), may hold values from -6 to 6
- occupations: float32 [4096], P('col'), may hold values from 0.02 to 1
Outputs:
- panel_coeffs: bfloat16 [2, 1024, 4096], P(None, 'row', 'col')
- density: bfloat16 [40960, 512], P(('row', 'col'))
Inputs may be any that keep to these rules, and one draw needn't show every extreme that they name: `tri_inverse`: each block is upper triangular with diagonal entries between 0.6 and 1.4.
All inputs are finite; a program needn't handle non-finite values.
Results may differ from a plain program's by a relative error of at most 0.025.
Values may be sent and summed in bfloat16 or wider, within the bound.
A program may use at most 128 MiB of HBM per device.

v0:
```python
import math

import jax
import jax.numpy as jnp
from jax import lax
from jax.sharding import Mesh
from jax.sharding import PartitionSpec as P

STATES = 4096
STRIP = 512
COL = ("col_0", "col_1")
ROW_COL = ("row", "col_0", "col_1")


def rows_first(arrays, axis, dims):
    turned = [jnp.moveaxis(a, dim, 0) for a, dim in zip(arrays, dims)]
    widths = [t[0].size for t in turned]
    both = jnp.concatenate([t.reshape(-1, w) for t, w in zip(turned, widths)], axis=1)
    filled = lax.all_gather(both, axis, axis=0, tiled=True)
    pieces = jnp.split(filled, [sum(widths[:k]) for k in range(1, len(widths))], axis=1)
    return tuple(
        (
            jnp.moveaxis(b.reshape(-1, *t.shape[1:]), 0, dim)
            for b, t, dim in zip(pieces, turned, dims)
        )
    )


def split_up(shard, dim, count):
    before, after = (shard.shape[:dim], shard.shape[dim + 1 :])
    return jnp.moveaxis(shard.reshape(*before, count, -1, *after), dim, 0)


def sum_at_owner(shard, axis, dim):
    count = lax.axis_size(axis)
    pieces = lax.all_to_all(split_up(shard, dim, count), axis, 0, 0, tiled=True)
    return jnp.sum(pieces.astype(jnp.float32), axis=0)


def copy_for_each(shard, axis):
    count = lax.axis_size(axis)
    return lax.all_to_all(
        jnp.broadcast_to(shard[None], (count, *shard.shape)), axis, 0, 0, tiled=True
    )


def joined_along(pieces, dim):
    pieces = jnp.moveaxis(pieces, 0, dim)
    lengths = pieces.shape
    return pieces.reshape(*lengths[:dim], lengths[dim] * lengths[dim + 1], *lengths[dim + 2 :])


def gathered_copies(shard, axis, dim):
    pieces = copy_for_each(shard, axis)
    return joined_along(pieces, dim)


def sum_by_axis(terms, axes):
    total = terms.astype(jnp.bfloat16)
    for axis in axes:
        total = lax.psum_scatter(total, axis, scatter_dimension=0, tiled=True)
    return total.astype(jnp.float32)


def apply_inverse(block_rows, share):
    return jnp.dot(
        block_rows,
        lax.all_gather(share, "row", axis=0, tiled=True),
        preferred_element_type=jnp.float32,
    )


def body(y_panels, tri_inverse, coupling, rest_factor, rest_coeffs, occupations):
    inverse_rows, coupling_rows = rows_first((tri_inverse, coupling), COL, (2, 1))
    flattened = rest_factor.reshape(rest_factor.shape[0], -1)
    partial_value = lax.dot_general(
        flattened, rest_coeffs, (((0,), (0,)), ((), ())), preferred_element_type=jnp.float32
    )
    partial_value = partial_value.reshape(2, -1, rest_coeffs.shape[1])
    update = sum_at_owner(partial_value.astype(jnp.bfloat16), "row", 1)
    second_rhs = (y_panels[1].astype(jnp.float32) - update[1]).astype(jnp.bfloat16)
    second = apply_inverse(inverse_rows[1], second_rhs).astype(jnp.bfloat16)
    cross = sum_at_owner(
        lax.dot_general(
            coupling_rows, second, (((0,), (0,)), ((), ())), preferred_element_type=jnp.float32
        ).astype(jnp.bfloat16),
        "row",
        0,
    )
    first_rhs = (y_panels[0].astype(jnp.float32) - update[0] - cross).astype(jnp.bfloat16)
    first = apply_inverse(inverse_rows[0], first_rhs).astype(jnp.bfloat16)
    panel_coeffs = jnp.stack([first, second])
    strip_block = gathered_copies(first, "row", 0)[:STRIP]
    factor_scale = 1.0 / math.sqrt(STATES)
    scaled = (strip_block.astype(jnp.float32) * (occupations * factor_scale)[None, :]).astype(
        jnp.bfloat16
    )
    density = sum_by_axis(
        lax.dot_general(
            rest_coeffs, scaled, (((1,), (1,)), ((), ())), preferred_element_type=jnp.float32
        ),
        COL,
    )
    return (panel_coeffs, density.astype(jnp.bfloat16))


def solution(mesh):
    finer = Mesh(mesh.devices.reshape(mesh.shape["row"], 4, 4), ("row", "col_0", "col_1"))
    placed = (
        P(None, "row", COL),
        P(None, "row", COL),
        P("row", COL),
        P("row", None, None),
        P("row", COL),
        P(COL),
    )
    return jax.shard_map(
        body,
        mesh=finer,
        in_specs=placed,
        out_specs=(P(None, "row", COL), P(ROW_COL, None)),
        check_vma=False,
    )
```

profile of v0, /device:TPU:1, one launch (start us, length us, event | category | flops | bytes accessed | tf_op | source)
XLA Modules:
  0.0 231.2 jit_solution(1781826063813069469)
XLA Ops:
  7.2 0.0 copy-start
  7.2 12.5 %copy.27 = bf16[320,8,2,1024]{3,1,2,0:T(8,128)(2,1)} copy(bf16[320,8,2,1024]{3,2,1,0:T(2,128)(2,1)} %bitcast.48) | data formatting | bytes 20971520
  19.7 13.8 %copy.18 = bf16[2048,2560]{1,0:T(8,128)(2,1)} copy(bf16[2048,2560]{0,1:T(8,128)(2,1)} %bitcast.47) | data formatting | bytes 20971520 | tf_op jit(solution)/shard_map/dot_general | solution.py:76
  33.5 0.0 copy-done
  33.5 6.9 %convolution_convert_fusion.1 = bf16[2,1024,256]{2,1,0:T(8,128)(2,1)S(1)} fusion(bf16[2,1024,2560]{2,1,0:T(8,128)(2,1)} %bitcast.49, bf16[2560,256]{1,0:T(8,128)(2,1)S(1)} %copy-done), kind=kOutput, calls=%fused_computation.3 | convolution fusion | flops 2684878848 | bytes 12845056 | tf_op jit(solution)/shard_map/dot_general | solution.py:76
  40.4 0.0 copy-start.3
  40.4 0.0 copy-start.2
  40.4 1.1 copy.29
  41.5 0.0 copy-start.1
  41.5 10.1 %all-to-all-start = ((bf16[16,2,64,256]{3,2,1,0:T(8,128)(2,1)}), bf16[16,2,64,256]{3,2,1,0:T(8,128)(2,1)S(1)}, u32[]{:S(2)}, u32[]{:S(2)}) async-start(bf16[16,2,64,256]{3,2,1,0:T(8,128)(2,1)} %bitcast.46), calls=%async_computation | async-start | bytes 2097152 | tf_op jit(solution)/shard_map/all_to_all | solution.py:36
  51.6 0.0 copy-done.3
  51.6 0.1 copy.16
  51.7 0.0 copy-done.2
  51.7 0.1 copy.21
  51.8 20.4 %all_gather.9 = bf16[1024,192]{1,0:T(8,128)(2,1)S(1)} all-gather(bf16[64,192]{1,0:T(8,128)(2,1)S(1)} %pad_maximum_fusion.1), channel_id=1, replica_groups=mesh['row'=16,'col_0'=4,'col_1'=4] {'col_0','col_1'}, dimensions={0}, use_global_device_ids=true | all-gather | bytes 417792 | tf_op jit(solution)/shard_map/all_gather | solution.py:19
  72.2 0.1 copy.26
  72.4 7.2 %all-to-all-done = bf16[16,2,64,256]{3,2,1,0:T(8,128)(2,1)S(1)} async-done(((bf16[16,2,64,256]{3,2,1,0:T(8,128)(2,1)}), bf16[16,2,64,256]{3,2,1,0:T(8,128)(2,1)S(1)}, u32[]{:S(2)}, u32[]{:S(2)}) %all-to-all-start) | async-done | bytes 1048608 | tf_op jit(solution)/shard_map/all_to_all | solution.py:36
  79.6 0.1 convert_reduce_fusion
  79.7 0.0 copy-done.1
  79.8 15.9 %all-gather = bf16[1,1024,256]{2,1,0:T(8,128)(2,1)S(1)} all-gather(bf16[1,64,256]{2,1,0:T(8,128)(2,1)S(1)} %fusion.7), channel_id=2, replica_groups=mesh['row'=16,'col_0'=4,'col_1'=4] {'row'}, dimensions={1}, use_global_device_ids=true | all-gather | bytes 557056 | tf_op jit(solution)/shard_map/all_gather | solution.py:68
  95.7 0.2 convolution_convert_fusion.4
  95.9 0.0 copy-start.4
  95.9 0.3 convolution_convert_fusion.2
  96.2 22.6 %all_to_all.15 = bf16[16,64,256]{2,1,0:T(8,128)(2,1)S(1)} all-to-all(bf16[16,64,256]{2,1,0:T(8,128)(2,1)S(1)} %bitcast.50), channel_id=1, replica_groups=mesh['row'=16,'col_0'=4,'col_1'=4] {'row'}, dimensions={0} | all-to-all | bytes 1048576 | tf_op jit(solution)/shard_map/all_to_all | solution.py:36
  118.8 0.1 convert_reduce_fusion.1
  118.9 15.9 %all_gather.11 = bf16[1024,256]{1,0:T(8,128)(2,1)S(1)} all-gather(bf16[64,256]{1,0:T(8,128)(2,1)S(1)} %fusion.10), channel_id=1, replica_groups=mesh['row'=16,'col_0'=4,'col_1'=4] {'row'}, dimensions={0}, use_global_device_ids=true | all-gather | bytes 557056 | tf_op jit(solution)/shard_map/all_gather | solution.py:68
  134.8 0.2 convolution_convert_fusion.3
  135.1 0.8 broadcast_in_dim.2
  135.9 5.2 %all-to-all-start.2 = ((bf16[16,64,256]{2,1,0:T(8,128)(2,1)}), bf16[16,64,256]{2,1,0:T(8,128)(2,1)S(1)}, u32[]{:S(2)}, u32[]{:S(2)}) async-start(bf16[16,64,256]{2,1,0:T(8,128)(2,1)} %broadcast_in_dim.2), calls=%async_computation.2 | async-start | bytes 1048576 | tf_op jit(solution)/shard_map/all_to_all | solution.py:42
  141.1 0.0 reduce-scatter.7.cloned.1.call-start
  141.1 0.0 copy-done.4
  141.2 17.1 %all-to-all-done.2 = bf16[16,64,256]{2,1,0:T(8,128)(2,1)S(1)} async-done(((bf16[16,64,256]{2,1,0:T(8,128)(2,1)}), bf16[16,64,256]{2,1,0:T(8,128)(2,1)S(1)}, u32[]{:S(2)}, u32[]{:S(2)}) %all-to-all-start.2) | async-done | bytes 524320 | tf_op jit(solution)/shard_map/all_to_all | solution.py:42
  158.3 2.4 %fusion = bf16[2560,512]{0,1:T(8,128)(2,1)} fusion(bf16[2560,256]{1,0:T(8,128)(2,1)S(1)} %copy-done, bf16[512,256]{1,0:T(8,128)(2,1)S(1)} %bitcast.51, f32[256]{0:T(256)S(1)} %broadcast_multiply_fusion), kind=kOutput, calls=%fused_computation.1 | convolution fusion | flops 672792576 | bytes 4195328 | tf_op jit(solution)/shard_map/dot_general | solution.py:99
  160.7 4.4 %copy.22 = bf16[2560,512]{1,0:T(8,128)(2,1)} copy(bf16[2560,512]{0,1:T(8,128)(2,1)} %fusion) | data formatting | bytes 5242880
  165.1 0.0 reduce-scatter.7.cloned.1.call-update
  165.1 0.0 reduce-scatter.9.cloned.1.call-start
  165.2 33.4 %reduce-scatter.7.cloned.1.call-done = bf16[640,512]{1,0:T(8,128)(2,1)} async-done(((bf16[2560,512]{1,0:T(8,128)(2,1)}), bf16[640,512]{1,0:T(8,128)(2,1)}) %reduce-scatter.7.cloned.1.call-update) | async-done | bytes 655376
  198.6 0.0 reduce-scatter.9.cloned.1.call-update
  198.6 0.6 pad_maximum_fusion
  199.3 25.1 %reduce-scatter.9.cloned.1.call-done = bf16[160,512]{1,0:T(8,128)(2,1)} async-done(((bf16[640,512]{1,0:T(8,128)(2,1)}), bf16[160,512]{1,0:T(8,128)(2,1)}) %reduce-scatter.9.cloned.1.call-update) | async-done | bytes 163856
  (6 shorter events, 0.1 us)
Async XLA Ops:
  7.2 26.4 %copy-start = (bf16[2560,256]{1,0:T(8,128)(2,1)S(1)}, bf16[2560,256]{1,0:T(8,128)(2,1)}, u32[]{:S(2)}) copy-start(bf16[2560,256]{1,0:T(8,128)(2,1)} %param.10) | copy-start | bytes 3932164
  40.4 11.2 %copy-start.3 = (bf16[64,64]{1,0:T(8,128)(2,1)S(1)}, bf16[64,64]{1,0:T(8,128)(2,1)}, u32[]{:S(2)}) copy-start(bf16[64,64]{1,0:T(8,128)(2,1)} %param.8) | copy-start | bytes 24580
  40.4 11.3 %copy-start.2 = (bf16[2,64,64]{2,1,0:T(8,128)(2,1)S(1)}, bf16[2,64,64]{2,1,0:T(8,128)(2,1)}, u32[]{:S(2)}) copy-start(bf16[2,64,64]{2,1,0:T(8,128)(2,1)} %param.7) | copy-start | bytes 49156
  41.5 38.3 %copy-start.1 = (bf16[2,64,256]{2,1,0:T(8,128)(2,1)S(1)}, bf16[2,64,256]{2,1,0:T(8,128)(2,1)}, u32[]{:S(2)}) copy-start(bf16[2,64,256]{2,1,0:T(8,128)(2,1)} %param.6) | copy-start | bytes 196612
  41.5 38.1 %all-to-all-start = ((bf16[16,2,64,256]{3,2,1,0:T(8,128)(2,1)}), bf16[16,2,64,256]{3,2,1,0:T(8,128)(2,1)S(1)}, u32[]{:S(2)}, u32[]{:S(2)}) async-start(bf16[16,2,64,256]{3,2,1,0:T(8,128)(2,1)} %bitcast.46), calls=%async_computation | async-start | bytes 2097152 | tf_op jit(solution)/shard_map/all_to_all | solution.py:36
  95.9 45.3 %copy-start.4 = (f32[256]{0:T(256)S(1)}, f32[256]{0:T(256)}, u32[]{:S(2)}) copy-start(f32[256]{0:T(256)} %param.11) | copy-start | bytes 3076
  135.9 22.4 %all-to-all-start.2 = ((bf16[16,64,256]{2,1,0:T(8,128)(2,1)}), bf16[16,64,256]{2,1,0:T(8,128)(2,1)S(1)}, u32[]{:S(2)}, u32[]{:S(2)}) async-start(bf16[16,64,256]{2,1,0:T(8,128)(2,1)} %broadcast_in_dim.2), calls=%async_computation.2 | async-start | bytes 1048576 | tf_op jit(solution)/shard_map/all_to_all | solution.py:42
  141.1 57.5 %reduce-scatter.7.cloned.1.call-start = ((), (), s32[]{:S(2)}) async-start(), calls=%async_computation.5 | async-start | bytes 3276800
  165.1 59.3 %reduce-scatter.9.cloned.1.call-start = ((), (), s32[]{:S(2)}) async-start(), calls=%async_computation.6 | async-start | bytes 819200
Sparse Core Ops, SparseCore 0:
  165.2 33.3 reduce-scatter.6
  201.7 22.6 reduce-scatter.8
where the time goes:
time: 233 us; the launch traced here: 231 us
  waiting for transfers between devices  82.9 us (36%)
  blocking collectives  74.8 us (32%)
  local copies, waits for them, and re-layouts  33 us (14%)
  starting transfers between devices  15.4 us (7%)
  between operations  14.2 us (6%)
  matrix products  9.95 us (4%)
    unnamed x4, waiting for transfers between devices  58.6 us
    all_gather x2, blocking collectives, apply_inverse(): lax.all_gather(share, 'row', axis=0, tiled=True)  31.8 us
    all_to_all x1, blocking collectives, sum_at_owner(): pieces = lax.all_to_all(split_up(shard, dim, count), axis, 0, 0, tiled=True)  22.6 us
    all_gather x1, blocking collectives, rows_first(): filled = lax.all_gather(both, axis, axis=0, tiled=True)  20.4 us
    unnamed x14, local copies, waits for them, and re-layouts  17.2 us
    all_to_all x1, waiting for transfers between devices, copy_for_each(): lax.all_to_all(jnp.broadcast_to(shard[None], (count, *shard.shape)), axis...  17.1 us
    dot_general x1, local copies, waits for them, and re-layouts, body(): lax.dot_general(flattened, rest_coeffs, (((0,), (0,)), ((), ())), preferr...  13.8 us
    all_to_all x1, starting transfers between devices, sum_at_owner(): pieces = lax.all_to_all(split_up(shard, dim, count), axis, 0, 0, tiled=True)  10.1 us
  transfers between devices with their start and end apart: 4, of which 4 were waited for; matrix products, arithmetic and copies ran while one was open for 0% of the time, Pallas kernels for 0%

commit v1 on v0

v1 whole, which is shorter than its diff:
```python
import jax
import jax.numpy as jnp
from jax import lax
from jax.experimental import pallas as pl
from jax.experimental.pallas import tpu as pltpu
from jax.sharding import PartitionSpec as P

MESH = pl.DeviceIdType.MESH
BF16 = jnp.bfloat16
F32 = jnp.float32
NZ = 8
SIDE = 4
KB = 256
CHUNKS = ((1, 0), (1, 1), (0, 0), (0, 1))
WIDE = 512


def iota(shape, dim):
    return lax.broadcasted_iota(jnp.int32, shape, dim)


def kernel(
    y_ref, tri_ref, coup_ref, fac_ref, rc_ref, occ_ref,
    panel_ref, dens_ref,
    fbuf, rci, tsend, trecv, tg, ownf, psend, precv, zsend, zrecv,
    sc, rca, rcb, pa, pb, paf, pbf, ra, rb, po, pr, turn,
    fsem, send_sem, recv_sem,
):
    r = lax.axis_index("row")
    c = lax.axis_index("col")
    z, core = r // 2, r % 2
    y, x = c // SIDE, c % SIDE
    rest = rc_ref.shape[0]
    count = [0]
    started = []

    def zdev(d, other=0):
        k = core if not other else 1 - core
        return (lax.rem(z + d, NZ) * 2 + k, c)

    def xcol(d):
        return y * SIDE + lax.rem(x + d, SIDE)

    def ycol(d):
        return lax.rem(y + d, SIDE) * SIDE + x

    def copy(src, dst, dev):
        k = count[0]
        count[0] += 1
        made = pltpu.make_async_remote_copy(
            src_ref=src, dst_ref=dst, send_sem=send_sem.at[k], recv_sem=recv_sem.at[k],
            device_id=dev, device_id_type=MESH,
        )
        made.start()
        started.append(made)
        return made

    partner = zdev(0, 1)

    loads = []
    for nb in range(8):
        load = pltpu.make_async_copy(
            fac_ref.at[:, :, pl.ds(nb * 128, 128)], fbuf.at[nb], fsem.at[nb]
        )
        loads.append(load)
    for nb in range(8):
        loads[nb].start()

    barrier = pltpu.get_barrier_semaphore()
    greeted = [partner]
    for d in range(1, NZ):
        greeted += [zdev(d), zdev(d, 1)]
    for d in range(1, SIDE):
        greeted += [(r, xcol(d)), (r, ycol(d))]
    for dev in greeted:
        pl.semaphore_signal(barrier, inc=1, device_id=dev, device_id_type=MESH)

    for m in range(3):
        block = (coup_ref[...] if m == 2 else tri_ref[m]).astype(F32).T.astype(BF16)
        tsend[m] = jnp.concatenate([block, block], axis=1)

    krow, kcol = iota((KB, 2 * KB), 0), iota((KB, 2 * KB), 1)
    spread = [jnp.where(kcol == 2 * krow + p, -1.0, 0.0).astype(BF16) for p in range(2)]

    def widen(kb, carry):
        turned = rc_ref[pl.ds(pl.multiple_of(kb * KB, KB), KB), :].T
        for p in range(2):
            rci[p, :, pl.ds(pl.multiple_of(kb * 2 * KB, 2 * KB), 2 * KB)] = jnp.dot(
                turned, spread[p], preferred_element_type=F32
            ).astype(BF16)
        return carry

    lax.fori_loop(0, rest // KB, widen, 0)

    pl.semaphore_wait(barrier, len(greeted))
    t_pair = copy(tsend, trecv, partner)

    def product(k):
        p, q = CHUNKS[k]
        if p == 1:
            for nb in range(4 * q, 4 * q + 4):
                loads[nb].wait()
        turned = y_ref[p].astype(F32).T.astype(BF16)
        here = core == 0

        def columns(n, carry):
            base = q * WIDE + n * 256
            place = (iota((64, 256), 1) + base == r * 64 + iota((64, 256), 0)).astype(F32)
            w = jnp.concatenate(
                [fbuf[4 * q + 2 * n + i].reshape(2 * rest, 128) for i in range(2)], axis=1
            )
            got = jnp.dot(rci[p], w, preferred_element_type=F32) + jnp.dot(
                turned, place.astype(BF16), preferred_element_type=F32
            )
            low, high = got[:128], got[128:]
            lanes = pl.ds(pl.multiple_of(n * 256, 256), 256)
            ownf[k, :, lanes] = jnp.where(here, low, high)
            psend[k, :, lanes] = jnp.where(here, high, low).astype(BF16)
            return carry

        lax.fori_loop(0, 2, columns, 0)
        return copy(psend.at[k], precv.at[k], partner)

    def combine(k, pair):
        pair.wait_recv()
        total = ownf[k] + precv[k].astype(F32)
        ownf[k] = total
        zsend[k] = total.astype(BF16).reshape(NZ, 16, WIDE)
        out = []
        for d in (4, 3, 5, 2, 6, 1, 7):
            out.append(copy(zsend.at[k, lax.rem(z + d, NZ)], zrecv.at[k, d], zdev(d)))
        return out

    pairs, zs = [], []
    pairs.append(product(0))

    t_pair.wait_recv()
    mine = (iota((32, 128), 1) // 64) == core
    for m in range(3):
        rows = pl.ds(core * 32, 32)
        tg[core, c, z, m] = jnp.where(
            mine, tsend[m, rows, :].astype(F32), trecv[m, rows, :].astype(F32)
        ).astype(BF16)
    t_z = [copy(tg.at[core, c, z], tg.at[core, c, z], zdev(d)) for d in (4, 3, 5, 2, 6, 1, 7)]

    pairs.append(product(1))
    zs.append(combine(0, pairs[0]))
    pairs.append(product(2))
    zs.append(combine(1, pairs[1]))

    for made in t_z:
        made.wait_recv()
    is0 = core == 0

    def slab(a, b):
        dx, dy = jnp.where(is0, a, b), jnp.where(is0, b, a)
        return lax.rem(y + dy, SIDE) * SIDE + lax.rem(x + dx, SIDE)

    t_a = [copy(tg.at[core, c], tg.at[core, c], (r, slab(d, 0))) for d in (2, 1, 3)]
    t_b = []
    for d in (2, 1, 3):
        t_b.append((d, 0, copy(tg.at[core, c], tg.at[core, c], (r, slab(0, d)))))

    pairs.append(product(3))
    zs.append(combine(2, pairs[2]))
    zs.append(combine(3, pairs[3]))

    t_d = [copy(tg.at[core, c], tg.at[core, c], partner)]
    for e, made in zip((2, 1, 3), t_a):
        made.wait_recv()
        came = slab(SIDE - e, 0)
        for d in (2, 1, 3):
            t_b.append((d, e, copy(tg.at[core, came], tg.at[core, came], (r, slab(0, d)))))
        t_d.append(copy(tg.at[core, came], tg.at[core, came], partner))

    view = rc_ref.reshape(SIDE, SIDE, 2, 80, 256)
    rc_x, rc_y = [], []
    for d in (2, 1, 3):
        rc_x.append(copy(view.at[:, lax.rem(x + d, SIDE), 0], rca.at[d], (r, xcol(d))))
        rc_y.append(copy(view.at[lax.rem(y + d, SIDE), :, 1], rcb.at[d], (r, ycol(d))))

    for d, e, made in t_b:
        made.wait_recv()
        came = slab((SIDE - e) % SIDE, SIDE - d)
        t_d.append(copy(tg.at[core, came], tg.at[core, came], partner))

    def rhs(p):
        parts = []
        for q in range(2):
            k = CHUNKS.index((p, q))
            for made in zs[k]:
                made.wait_recv()
            total = ownf[k, pl.ds(z * 16, 16), :]
            for d in range(1, NZ):
                total = total + zrecv[k, d].astype(F32)
            parts.append(total)
        return jnp.concatenate(parts, axis=1)

    def tile(m, kb, zs_):
        cols = []
        for zz in zs_:
            cols.append(
                jnp.concatenate(
                    [tg[h, cc, zz, m] for cc in range(4 * kb, 4 * kb + 4) for h in range(2)], axis=0
                )
            )
        return jnp.concatenate(cols, axis=1)

    def upper(m, value, q):
        total = None
        for kb in range(q, 4):
            part = jnp.dot(
                value[:, kb * 256:(kb + 1) * 256], tile(m, kb, (2 * q, 2 * q + 1)),
                preferred_element_type=F32,
            )
            total = part if total is None else total + part
        return total

    rhs1 = rhs(1).astype(BF16)
    for made in t_d:
        made.wait_recv()
    second = jnp.concatenate([upper(1, rhs1, q) for q in range(4)], axis=1).astype(BF16)
    cross = jnp.concatenate(
        [
            lax.dot_general(
                second, tile(2, kb, range(8)), (((1,), (1,)), ((), ())), preferred_element_type=F32
            )
            for kb in range(4)
        ],
        axis=1,
    )
    rhs0 = (rhs(0) - cross).astype(BF16)
    strip = jnp.concatenate([upper(0, rhs0, q) for q in range(2)], axis=1).astype(BF16)

    lane = iota((16, 256), 1)
    wanted = core * 128 + z * 16 + iota((16, 256), 0)
    weight = jnp.sum(jnp.where(lane == wanted, occ_ref[...], 0.0), axis=1, keepdims=True)
    sc[0, core, z] = (strip.astype(F32) * (weight * 0.015625)).astype(BF16)

    s_z, s_x, s_y = [], [], []
    for d in (1, 7, 2, 6, 3, 5, 4):
        s_z.append((d, copy(sc.at[0, core, z], sc.at[0, core, z], zdev(d))))

    def spread_out(zz):
        for d in (2, 1, 3):
            s_x.append(copy(sc.at[0, core, zz], sc.at[d, core, zz], (r, xcol(d))))
            s_y.append(copy(sc.at[0, core, zz], sc.at[3 + d, core, zz], (r, ycol(d))))

    spread_out(z)

    tail = jnp.concatenate([upper(0, rhs0, q) for q in range(2, 4)], axis=1).astype(BF16)
    first = jnp.concatenate([strip, tail], axis=1)
    for zz in range(NZ):
        po[zz, 0] = first[:, zz * 128:(zz + 1) * 128]
        po[zz, 1] = second[:, zz * 128:(zz + 1) * 128]
    pr[core, z] = po[z]

    for d, made in s_z:
        made.wait_recv()
        spread_out(lax.rem(z + NZ - d, NZ))
    s_d = [copy(sc.at[0, core], sc.at[0, core], partner)]

    p_out = []
    for d in range(NZ):
        for other in range(2):
            if d or other:
                dev = zdev(d, other)
                p_out.append(copy(po.at[lax.rem(z + d, NZ)], pr.at[core, z], dev))

    for g, made in zip((2, 1, 3) * NZ, s_x):
        made.wait_recv()
    for g in (2, 1, 3):
        s_d.append(copy(sc.at[g, core], sc.at[g, core], partner))
    for g, made in zip((2, 1, 3) * NZ, s_y):
        made.wait_recv()
    for g in (2, 1, 3):
        s_d.append(copy(sc.at[3 + g, core], sc.at[3 + g, core], partner))
    for made in rc_x:
        made.wait_recv()
    for made in s_d:
        made.wait_recv()
    total = jnp.dot(view[:, x, 0].reshape(320, 256), sc[0].reshape(256, 512), preferred_element_type=F32)
    for d in range(1, SIDE):
        total = total + jnp.dot(
            rca[d].reshape(320, 256), sc[d].reshape(256, 512), preferred_element_type=F32
        )
    paf[...] = total.reshape(SIDE, 80, 512)
    pa[...] = total.astype(BF16).reshape(SIDE, 80, 512)
    r_y = [copy(pa.at[lax.rem(y + d, SIDE)], ra.at[d], (r, ycol(d))) for d in (2, 1, 3)]
    for made in rc_y:
        made.wait_recv()
    total = jnp.dot(view[y, :, 1].reshape(320, 256), sc[0].reshape(256, 512), preferred_element_type=F32)
    for d in range(1, SIDE):
        total = total + jnp.dot(
            rcb[d].reshape(320, 256), sc[3 + d].reshape(256, 512), preferred_element_type=F32
        )
    pbf[...] = total.reshape(SIDE, 80, 512)
    pb[...] = total.astype(BF16).reshape(SIDE, 80, 512)
    r_x = [copy(pb.at[lax.rem(x + d, SIDE)], rb.at[d], (r, xcol(d))) for d in (2, 1, 3)]

    for made in p_out:
        made.wait_recv()
    for p in range(2):
        states = jnp.concatenate([pr[k, zz, p] for k in range(2) for zz in range(NZ)], axis=0)
        turn[p] = states.astype(F32).T
        panel_ref[p] = turn[p, pl.ds(core * 64, 64), :].astype(BF16)

    for made in r_y:
        made.wait_recv()
    total = paf[y]
    for d in range(1, SIDE):
        total = total + ra[d].astype(F32)
    dens_ref[pl.ds(0, 80), :] = total.astype(BF16)
    for made in r_x:
        made.wait_recv()
    total = pbf[x]
    for d in range(1, SIDE):
        total = total + rb[d].astype(F32)
    dens_ref[pl.ds(80, 80), :] = total.astype(BF16)

    for made in started:
        made.wait_send()


def body(y_panels, tri_inverse, coupling, rest_factor, rest_coeffs, occupations):
    rest = rest_coeffs.shape[0]
    vmem = pl.BlockSpec(memory_space=pltpu.VMEM)
    anywhere = pl.BlockSpec(memory_space=pl.ANY)
    copies = 180
    return pl.pallas_call(
        kernel,
        out_shape=(
            jax.ShapeDtypeStruct((2, 64, 256), BF16),
            jax.ShapeDtypeStruct((160, 512), BF16),
        ),
        in_specs=[vmem, vmem, vmem, anywhere, vmem, vmem],
        out_specs=(vmem, vmem),
        scratch_shapes=[
            pltpu.VMEM((8, rest, 2, 128), BF16),
            pltpu.VMEM((2, 256, 2 * rest), BF16),
            pltpu.VMEM((3, 64, 128), BF16),
            pltpu.VMEM((3, 64, 128), BF16),
            pltpu.VMEM((2, 16, NZ, 3, 32, 128), BF16),
            pltpu.VMEM((4, 128, WIDE), F32),
            pltpu.VMEM((4, 128, WIDE), BF16),
            pltpu.VMEM((4, 128, WIDE), BF16),
            pltpu.VMEM((4, NZ, 16, WIDE), BF16),
            pltpu.VMEM((4, NZ, 16, WIDE), BF16),
            pltpu.VMEM((7, 2, NZ, 16, 512), BF16),
            pltpu.VMEM((SIDE, SIDE, 80, 256), BF16),
            pltpu.VMEM((SIDE, SIDE, 80, 256), BF16),
            pltpu.VMEM((SIDE, 80, 512), BF16),
            pltpu.VMEM((SIDE, 80, 512), BF16),
            pltpu.VMEM((SIDE, 80, 512), F32),
            pltpu.VMEM((SIDE, 80, 512), F32),
            pltpu.VMEM((SIDE, 80, 512), BF16),
            pltpu.VMEM((SIDE, 80, 512), BF16),
            pltpu.VMEM((NZ, 2, 16, 128), BF16),
            pltpu.VMEM((2, NZ, 2, 16, 128), BF16),
            pltpu.VMEM((2, 128, 256), F32),
            pltpu.SemaphoreType.DMA((8,)),
            pltpu.SemaphoreType.DMA((copies,)),
            pltpu.SemaphoreType.DMA((copies,)),
        ],
        compiler_params=pltpu.CompilerParams(
            collective_id=0, has_side_effects=True, vmem_limit_bytes=60 * 1024 * 1024
        ),
    )(y_panels, tri_inverse, coupling, rest_factor, rest_coeffs, occupations.reshape(1, 256))


def solution(mesh):
    return jax.shard_map(
        body,
        mesh=mesh,
        in_specs=(
            P(None, "row", "col"),
            P(None, "row", "col"),
            P("row", "col"),
            P("row", None, None),
            P("row", "col"),
            P("col"),
        ),
        out_specs=(P(None, "row", "col"), P(("row", "col"), None)),
        check_vma=False,
    )
```

time: 233 us -> 78.6 us (0.34)
  waiting for transfers between devices: 82.9 us -> 0 us
  blocking collectives: 74.8 us -> 0 us
  Pallas kernels: 0 us -> 74.7 us
  local copies, waits for them, and re-layouts: 33 us -> 3.07 us
  starting transfers between devices: 15.4 us -> 0 us
  between operations: 14.2 us -> 0.64 us
  matrix products: 9.95 us -> 0 us
    pallas_call x0 -> x1, Pallas kernels: none -> 74.7 us  [body(): pl.pallas_call(kernel, out_shape=(jax.ShapeDtypeStruct((2, 64, 256), BF16...]
    unnamed x4 -> x0, waiting for transfers between devices: 58.6 us -> none
    all_gather x3 -> x0, blocking collectives: 52.2 us -> none  [the longest x2 31.8 us: apply_inverse(): lax.all_gather(share, 'row', axis=0, tiled=True)]
    all_to_all x2 -> x0, waiting for transfers between devices: 24.4 us -> none  [the longest x1 17.1 us: copy_for_each(): lax.all_to_all(jnp.broadcast_to(shard[None], (count, *shard.shape)), axis...]
    all_to_all x1 -> x0, blocking collectives: 22.6 us -> none  [sum_at_owner(): pieces = lax.all_to_all(split_up(shard, dim, count), axis, 0, 0, tiled=True)]
    all_to_all x2 -> x0, starting transfers between devices: 15.3 us -> none  [the longest x1 10.1 us: sum_at_owner(): pieces = lax.all_to_all(split_up(shard, dim, count), axis, 0, 0, tiled=True)]
    unnamed x14 -> x2, local copies, waits for them, and re-layouts: 17.2 us -> 3.07 us
    dot_general x1 -> x0, local copies, waits for them, and re-layouts: 13.8 us -> none  [body(): lax.dot_general(flattened, rest_coeffs, (((0,), (0,)), ((), ())), preferr...]
  transfers between devices with their start and end apart: 4 -> 0, of which waited for: 4 -> 0; matrix products, arithmetic and copies ran while one was open for 0% -> 0% of each run, Pallas kernels for 0% -> 0%
where the time goes in v1:
time: 78.6 us; the launch traced here: 78.4 us
  Pallas kernels  74.7 us (95%)
  local copies, waits for them, and re-layouts  3.07 us (4%)
    pallas_call x1, Pallas kernels, body(): pl.pallas_call(kernel, out_shape=(jax.ShapeDtypeStruct((2, 64, 256), BF16...  74.7 us
    unnamed x2, local copies, waits for them, and re-layouts  3.07 us

profile of v1, /device:TPU:1, one launch (start us, length us, event | category | flops | bytes accessed | tf_op | source)
XLA Modules:
  0.0 78.4 jit_solution(2837408013013450167)
XLA Ops:
  0.6 74.7 %shard_map.77 = (bf16[2,64,256]{2,1,0:T(8,128)(2,1)}, bf16[160,512]{1,0:T(8,128)(2,1)}) custom-call(bf16[2,64,256]{2,1,0:T(8,128)(2,1)} %y_ref.1, bf16[2,64,64]{2,1,0:T(8,128)(2,1)} %tri_ref.1, bf16[64,64]{1,0:T(8,128)(2,1)} %coup_ref.1, bf16[2560,2,1024]{2,1,0:T(2,128)(2,1)} %fac_ref.1, bf16[2560,256]{1,0:T(8,128)(2,1)} %rc_ref.1, f32[1,256]{1,0:T(1,128)} %bitcast.1), custom_call_target="tpu_custom_call" | custom-call | tf_op jit(solution)/shard_map/pallas_call | solution.py:330
  75.4 1.5 %copy.10 = bf16[2,64,256]{2,1,0:T(8,128)(2,1)} copy(bf16[2,64,256]{2,1,0:T(8,128)(2,1)} %get-tuple-element.4) | data formatting | bytes 131072
  76.9 1.6 %copy.11 = bf16[160,512]{1,0:T(8,128)(2,1)} copy(bf16[160,512]{1,0:T(8,128)(2,1)} %get-tuple-element.5) | data formatting | bytes 327680

commit v2 on v1

v2 whole, which is shorter than its diff:
```python
import jax
import jax.numpy as jnp
from jax import lax
from jax.experimental import pallas as pl
from jax.experimental.pallas import tpu as pltpu
from jax.sharding import PartitionSpec as P

MESH = pl.DeviceIdType.MESH
BF16 = jnp.bfloat16
F32 = jnp.float32
NZ = 8
SIDE = 4
KB = 256
CHUNKS = ((1, 0), (1, 1), (0, 0), (0, 1))
WIDE = 512


def iota(shape, dim):
    return lax.broadcasted_iota(jnp.int32, shape, dim)


def kernel(
    y_in, tri_in, coup_in, fac_ref, rc_in, occ_in,
    panel_ref, dens_ref,
    y_ref, tri_ref, coup_ref, rc_ref, occ_ref,
    fbuf, rci, tsend, trecv, tt, cg, ownf, psend, precv, zsend, zrecv,
    sc, rca, rcb, pa, pb, paf, pbf, ra, rb, po, pr, turn,
    fsem, send_sem, recv_sem,
):
    r = lax.axis_index("row")
    c = lax.axis_index("col")
    z, core = r // 2, r % 2
    y, x = c // SIDE, c % SIDE
    rest = rc_ref.shape[0]
    count = [0]
    started = []

    def zdev(d, other=0):
        k = core if not other else 1 - core
        return (lax.rem(z + d, NZ) * 2 + k, c)

    def xcol(d):
        return y * SIDE + lax.rem(x + d, SIDE)

    def ycol(d):
        return lax.rem(y + d, SIDE) * SIDE + x

    def copy(src, dst, dev):
        k = count[0]
        count[0] += 1
        made = pltpu.make_async_remote_copy(
            src_ref=src, dst_ref=dst, send_sem=send_sem.at[k], recv_sem=recv_sem.at[k],
            device_id=dev, device_id_type=MESH,
        )
        made.start()
        started.append(made)
        return made

    partner = zdev(0, 1)

    barrier = pltpu.get_barrier_semaphore()
    greeted = [partner]
    for d in range(1, NZ):
        greeted += [zdev(d), zdev(d, 1)]
    for d in range(1, SIDE):
        greeted += [(r, xcol(d)), (r, ycol(d))]
    for dev in greeted:
        pl.semaphore_signal(barrier, inc=1, device_id=dev, device_id_type=MESH)

    own = []
    for k, (src, dst) in enumerate(
        ((tri_in, tri_ref), (coup_in, coup_ref), (rc_in, rc_ref), (y_in, y_ref), (occ_in, occ_ref))
    ):
        own.append(pltpu.make_async_copy(src, dst, fsem.at[8 + k]))
        own[k].start()

    loads = []
    for nb in range(8):
        load = pltpu.make_async_copy(
            fac_ref.reshape(2 * rest, 1024).at[:, pl.ds(nb * 128, 128)], fbuf.at[nb], fsem.at[nb]
        )
        loads.append(load)
    for nb in range(8):
        loads[nb].start()

    own[0].wait()
    own[1].wait()
    for m in range(3):
        block = (coup_ref[...] if m == 2 else tri_ref[m]).astype(F32).T.astype(BF16)
        tsend[m] = jnp.concatenate([block, block], axis=1)

    own[2].wait()
    krow, kcol = iota((KB, 2 * KB), 0), iota((KB, 2 * KB), 1)
    spread = [jnp.where(kcol == 2 * krow + p, -1.0, 0.0).astype(BF16) for p in range(2)]

    def widen(kb, carry):
        turned = rc_ref[pl.ds(pl.multiple_of(kb * KB, KB), KB), :].T
        for p in range(2):
            rci[p, :, pl.ds(pl.multiple_of(kb * 2 * KB, 2 * KB), 2 * KB)] = jnp.dot(
                turned, spread[p], preferred_element_type=F32
            ).astype(BF16)
        return carry

    half = rest // KB // 2
    lax.fori_loop(0, half, widen, 0)

    pl.semaphore_wait(barrier, len(greeted))
    t_pair = copy(tsend, trecv, partner)

    view = rc_ref.reshape(SIDE, SIDE, 2, 80, 256)
    rc_x, rc_y = [], []

    def exchange(d):
        rc_x.append(copy(view.at[:, lax.rem(x + d, SIDE), 0], rca.at[d], (r, xcol(d))))
        rc_y.append(copy(view.at[lax.rem(y + d, SIDE), :, 1], rcb.at[d], (r, ycol(d))))

    for d in (2, 1, 3):
        exchange(d)

    def product(k):
        p, q = CHUNKS[k]
        if p == 1:
            for nb in range(4 * q, 4 * q + 4):
                loads[nb].wait()
        if k == 0:
            own[3].wait()
        turned = y_ref[p].astype(F32).T.astype(BF16)
        here = core == 0

        def columns(n, carry):
            base = q * WIDE + n * 256
            place = (iota((64, 256), 1) + base == r * 64 + iota((64, 256), 0)).astype(F32)
            w = jnp.concatenate([fbuf[4 * q + 2 * n + i] for i in range(2)], axis=1)
            got = jnp.dot(rci[p], w, preferred_element_type=F32) + jnp.dot(
                turned, place.astype(BF16), preferred_element_type=F32
            )
            low, high = got[:128], got[128:]
            lanes = pl.ds(pl.multiple_of(n * 256, 256), 256)
            ownf[k, :, lanes] = jnp.where(here, low, high)
            psend[k, :, lanes] = jnp.where(here, high, low).astype(BF16)
            return carry

        lax.fori_loop(0, 2, columns, 0)
        return copy(psend.at[k], precv.at[k], partner)

    def combine(k, pair):
        pair.wait_recv()
        total = ownf[k] + precv[k].astype(F32)
        ownf[k] = total
        zsend[k] = total.astype(BF16).reshape(NZ, 16, WIDE)
        out = []
        for d in (4, 3, 5, 2, 6, 1, 7):
            out.append(copy(zsend.at[k, lax.rem(z + d, NZ)], zrecv.at[k, d], zdev(d)))
        return out

    pairs, zs = [], []
    is0 = core == 0

    class Upper:
        def __init__(self, cc, to, out, come):
            k = count[0]
            count[0] += 1
            self.out, self.come = out, come
            self.made = [
                pltpu.make_async_remote_copy(
                    src_ref=tt.at[core, cc, pl.ds(0, 2 * v + 2)],
                    dst_ref=tt.at[core, cc, pl.ds(0, 2 * v + 2)],
                    send_sem=send_sem.at[k], recv_sem=recv_sem.at[k],
                    device_id=to, device_id_type=MESH,
                )
                for v in range(SIDE)
            ]
            for v in range(SIDE):
                pl.when(out == v)(self.made[v].start)
            started.append(self)

        def wait_recv(self):
            for v in range(SIDE):
                pl.when(self.come == v)(self.made[v].wait_recv)

        def wait_send(self):
            for v in range(SIDE):
                pl.when(self.out == v)(self.made[v].wait_send)

    def whole(cc, to):
        return copy(cg.at[core, cc], cg.at[core, cc], to)

    class Maybe:
        def __init__(self, src, dst, to, out, come):
            k = count[0]
            count[0] += 1
            self.out, self.come = out, come
            self.made = pltpu.make_async_remote_copy(
                src_ref=src, dst_ref=dst, send_sem=send_sem.at[k], recv_sem=recv_sem.at[k],
                device_id=to, device_id_type=MESH,
            )
            pl.when(out)(self.made.start)
            started.append(self)

        def wait_recv(self):
            pl.when(self.come)(self.made.wait_recv)

        def wait_send(self):
            pl.when(self.out)(self.made.wait_send)

    t_pair.wait_recv()
    mine = (iota((32, 128), 1) // 64) == core
    for m in range(3):
        rows = pl.ds(core * 32, 32)
        got = jnp.where(
            mine, tsend[m, rows, :].astype(F32), trecv[m, rows, :].astype(F32)
        ).astype(BF16)
        if m == 2:
            cg[core, c, z] = got
        else:
            tt[core, c, z, m] = got
    t_z = []
    for d in (4, 3, 5, 2, 6, 1, 7):
        t_z.append(copy(cg.at[core, c, z], cg.at[core, c, z], zdev(d)))
        t_z.append(
            Maybe(
                tt.at[core, c, z], tt.at[core, c, z], zdev(d),
                z <= 2 * y + 1, lax.rem(z + NZ - d, NZ) <= 2 * y + 1,
            )
        )

    def moved(a, b):
        dx, dy = jnp.where(is0, a, b), jnp.where(is0, b, a)
        return lax.rem(x + dx, SIDE), lax.rem(y + dy, SIDE)

    def slab(a, b):
        xx, yy = moved(a, b)
        return yy * SIDE + xx

    def behind(e, d):
        back = ((SIDE - e) % SIDE, (SIDE - d) % SIDE)
        return slab(*back), moved(*back)[1], moved(*back[::-1])[1]

    def to_axis_b(e):
        cc, out, _ = behind(e, 0)
        for d in (1, 3):
            to = (r, slab(0, d))
            t_b[e, d] = (Upper(cc, to, out, behind(e, d)[1]), whole(cc, to))
        to_partner(e, 0)

    def onward(e):
        for made in t_b[e, 1] + t_b[e, 3]:
            made.wait_recv()
        far = behind(e, 2)[1]
        t_far[e] = (
            Upper(behind(e, 3)[0], (r, slab(0, 3)), behind(e, 3)[1], far),
            whole(behind(e, 1)[0], (r, slab(0, 1))),
        )
        to_partner(e, 1)
        to_partner(e, 3)

    def to_partner(e, d):
        cc, out, come = behind(e, d)
        t_d.append(Upper(cc, partner, out, come))
        t_d.append(whole(cc, partner))

    lax.fori_loop(half, rest // KB, widen, 0)
    pairs.append(product(0))
    pairs.append(product(1))

    for made in t_z:
        made.wait_recv()
    t_a, t_b, t_far, t_d = {}, {}, {}, []
    for d in (1, 3, 2):
        to = (r, slab(d, 0))
        t_a[d] = (Upper(c, to, y, behind(d, 0)[1]), whole(c, to))

    zs.append(combine(0, pairs[0]))
    zs.append(combine(1, pairs[1]))
    pairs.append(product(2))
    pairs.append(product(3))
    to_axis_b(0)
    zs.append(combine(2, pairs[2]))

    for e in (1, 3, 2):
        for made in t_a[e]:
            made.wait_recv()
        to_axis_b(e)
        if e == 1:
            zs.append(combine(3, pairs[3]))
        if e == 3:
            onward(0)
    for e in (1, 3, 2):
        onward(e)
    for e in (0, 1, 3, 2):
        for made in t_far[e]:
            made.wait_recv()
        to_partner(e, 2)

    def rhs(p):
        parts = []
        for q in range(2):
            k = CHUNKS.index((p, q))
            for made in zs[k]:
                made.wait_recv()
            total = ownf[k, pl.ds(z * 16, 16), :]
            for d in range(1, NZ):
                total = total + zrecv[k, d].astype(F32)
            parts.append(total)
        return jnp.concatenate(parts, axis=1)

    def tile(m, kb, zs_):
        cols = []
        for zz in zs_:
            cols.append(
                jnp.concatenate(
                    [cg[h, cc, zz] if m == 2 else tt[h, cc, zz, m] for cc in range(4 * kb, 4 * kb + 4) for h in range(2)], axis=0
                )
            )
        return jnp.concatenate(cols, axis=1)

    def upper(m, value, q):
        total = None
        for kb in range(q, 4):
            part = jnp.dot(
                value[:, kb * 256:(kb + 1) * 256], tile(m, kb, (2 * q, 2 * q + 1)),
                preferred_element_type=F32,
            )
            total = part if total is None else total + part
        return total

    rhs1 = rhs(1).astype(BF16)
    for made in t_d:
        made.wait_recv()
    second = jnp.concatenate([upper(1, rhs1, q) for q in range(4)], axis=1).astype(BF16)
    cross = jnp.concatenate(
        [
            lax.dot_general(
                second, tile(2, kb, range(8)), (((1,), (1,)), ((), ())), preferred_element_type=F32
            )
            for kb in range(4)
        ],
        axis=1,
    )
    rhs0 = (rhs(0) - cross).astype(BF16)
    strip = jnp.concatenate([upper(0, rhs0, q) for q in range(2)], axis=1).astype(BF16)

    own[4].wait()
    lane = iota((16, 256), 1)
    wanted = core * 128 + z * 16 + iota((16, 256), 0)
    weight = jnp.sum(jnp.where(lane == wanted, occ_ref[...], 0.0), axis=1, keepdims=True)
    sc[0, core, z] = (strip.astype(F32) * (weight * 0.015625)).astype(BF16)

    s_z, s_x, s_y = [], [], []
    for d in (4, 3, 5, 2, 6, 1, 7):
        s_z.append((d, copy(sc.at[0, core, z], sc.at[0, core, z], zdev(d))))

    def spread_out(zz, zin):
        for d in (2, 1, 3):
            s_x.append((d, zin, copy(sc.at[0, core, zz], sc.at[d, core, zz], (r, xcol(d)))))
            s_y.append((3 + d, zin, copy(sc.at[0, core, zz], sc.at[3 + d, core, zz], (r, ycol(d)))))

    spread_out(z, z)

    tail = jnp.concatenate([upper(0, rhs0, q) for q in range(2, 4)], axis=1).astype(BF16)
    first = jnp.concatenate([strip, tail], axis=1)
    for zz in range(NZ):
        po[zz, 0] = first[:, zz * 128:(zz + 1) * 128]
        po[zz, 1] = second[:, zz * 128:(zz + 1) * 128]
    pr[core, z] = po[z]

    for d, made in s_z[::-1]:
        made.wait_recv()
        zz = lax.rem(z + NZ - d, NZ)
        spread_out(zz, zz)
    s_d = [copy(sc.at[0, core], sc.at[0, core], partner)]

    p_out = []
    for d in range(NZ):
        for other in range(2):
            if d or other:
                dev = zdev(d, other)
                p_out.append(copy(po.at[lax.rem(z + d, NZ)], pr.at[core, z], dev))

    for pair in zip(s_x, s_y):
        for g, zz, made in pair:
            made.wait_recv()
            s_d.append(copy(sc.at[g, core, zz], sc.at[g, core, zz], partner))
    for made in rc_x + rc_y + s_d:
        made.wait_recv()

    def along_y(steps):
        rows = [lax.rem(y + d, SIDE) for d in steps]
        total = 0.0
        for g in range(SIDE):
            block = jnp.concatenate([rca[g, k] if g else view[k, x, 0] for k in rows], axis=0)
            total = total + jnp.dot(block, sc[g].reshape(256, 512), preferred_element_type=F32)
        return total

    def along_x(steps):
        rows = [lax.rem(x + d, SIDE) for d in steps]
        total = 0.0
        for g in range(SIDE):
            block = jnp.concatenate([rcb[g, k] if g else view[y, k, 1] for k in rows], axis=0)
            slot = 3 + g if g else 0
            total = total + jnp.dot(block, sc[slot].reshape(256, 512), preferred_element_type=F32)
        return total

    far = (2, 1, 3)
    pa[...] = along_y(far).astype(BF16).reshape(3, 80, 512)
    r_y = [copy(pa.at[k], ra.at[d], (r, ycol(d))) for k, d in enumerate(far)]
    pb[...] = along_x(far).astype(BF16).reshape(3, 80, 512)
    r_x = [copy(pb.at[k], rb.at[d], (r, xcol(d))) for k, d in enumerate(far)]
    paf[...] = along_y((0,))
    pbf[...] = along_x((0,))

    for made in p_out:
        made.wait_recv()
    for p in range(2):
        states = jnp.concatenate([pr[k, zz, p] for k in range(2) for zz in range(NZ)], axis=0)
        turn[p] = states.astype(F32).T
        panel_ref[p] = turn[p, pl.ds(core * 64, 64), :].astype(BF16)

    for made in r_y:
        made.wait_recv()
    total = paf[...]
    for d in range(1, SIDE):
        total = total + ra[d].astype(F32)
    dens_ref[pl.ds(0, 80), :] = total.astype(BF16)
    for made in r_x:
        made.wait_recv()
    total = pbf[...]
    for d in range(1, SIDE):
        total = total + rb[d].astype(F32)
    dens_ref[pl.ds(80, 80), :] = total.astype(BF16)

    for made in started:
        made.wait_send()


def body(y_panels, tri_inverse, coupling, rest_factor, rest_coeffs, occupations):
    rest = rest_coeffs.shape[0]
    vmem = pl.BlockSpec(memory_space=pltpu.VMEM)
    anywhere = pl.BlockSpec(memory_space=pltpu.HBM)
    copies = 300
    return pl.pallas_call(
        kernel,
        out_shape=(
            jax.ShapeDtypeStruct((2, 64, 256), BF16),
            jax.ShapeDtypeStruct((160, 512), BF16),
        ),
        in_specs=[anywhere] * 6,
        out_specs=(vmem, vmem),
        scratch_shapes=[
            pltpu.VMEM((2, 64, 256), BF16),
            pltpu.VMEM((2, 64, 64), BF16),
            pltpu.VMEM((64, 64), BF16),
            pltpu.VMEM((rest, 256), BF16),
            pltpu.VMEM((1, 256), F32),
            pltpu.VMEM((8, 2 * rest, 128), BF16),
            pltpu.VMEM((2, 256, 2 * rest), BF16),
            pltpu.VMEM((3, 64, 128), BF16),
            pltpu.VMEM((3, 64, 128), BF16),
            pltpu.VMEM((2, 16, NZ, 2, 32, 128), BF16),
            pltpu.VMEM((2, 16, NZ, 32, 128), BF16),
            pltpu.VMEM((4, 128, WIDE), F32),
            pltpu.VMEM((4, 128, WIDE), BF16),
            pltpu.VMEM((4, 128, WIDE), BF16),
            pltpu.VMEM((4, NZ, 16, WIDE), BF16),
            pltpu.VMEM((4, NZ, 16, WIDE), BF16),
            pltpu.VMEM((7, 2, NZ, 16, 512), BF16),
            pltpu.VMEM((SIDE, SIDE, 80, 256), BF16),
            pltpu.VMEM((SIDE, SIDE, 80, 256), BF16),
            pltpu.VMEM((3, 80, 512), BF16),
            pltpu.VMEM((3, 80, 512), BF16),
            pltpu.VMEM((80, 512), F32),
            pltpu.VMEM((80, 512), F32),
            pltpu.VMEM((SIDE, 80, 512), BF16),
            pltpu.VMEM((SIDE, 80, 512), BF16),
            pltpu.VMEM((NZ, 2, 16, 128), BF16),
            pltpu.VMEM((2, NZ, 2, 16, 128), BF16),
            pltpu.VMEM((2, 128, 256), F32),
            pltpu.SemaphoreType.DMA((13,)),
            pltpu.SemaphoreType.DMA((copies,)),
            pltpu.SemaphoreType.DMA((copies,)),
        ],
        compiler_params=pltpu.CompilerParams(
            collective_id=0, has_side_effects=True, vmem_limit_bytes=60 * 1024 * 1024
        ),
    )(y_panels, tri_inverse, coupling, rest_factor, rest_coeffs, occupations.reshape(1, 256))


def solution(mesh):
    return jax.shard_map(
        body,
        mesh=mesh,
        in_specs=(
            P(None, "row", "col"),
            P(None, "row", "col"),
            P("row", "col"),
            P("row", None, None),
            P("row", "col"),
            P("col"),
        ),
        out_specs=(P(None, "row", "col"), P(("row", "col"), None)),
        check_vma=False,
    )
```

time: 78.6 us -> 70.8 us (0.901)
  Pallas kernels: 74.7 us -> 66.9 us
    pallas_call x1, Pallas kernels: 74.7 us -> 66.9 us  [body(): pl.pallas_call(kernel, out_shape=(jax.ShapeDtypeStruct((2, 64, 256), BF16...]
where the time goes in v2:
time: 70.8 us; the launch traced here: 70.6 us
  Pallas kernels  66.9 us (94%)
  local copies, waits for them, and re-layouts  3.07 us (4%)
    pallas_call x1, Pallas kernels, body(): pl.pallas_call(kernel, out_shape=(jax.ShapeDtypeStruct((2, 64, 256), BF16...  66.9 us
    unnamed x2, local copies, waits for them, and re-layouts  3.07 us

profile of v2, /device:TPU:1, one launch (start us, length us, event | category | flops | bytes accessed | tf_op | source)
XLA Modules:
  0.0 70.6 jit_solution(1929485065800377470)
XLA Ops:
  0.6 66.9 %shard_map.77 = (bf16[2,64,256]{2,1,0:T(8,128)(2,1)}, bf16[160,512]{1,0:T(8,128)(2,1)}) custom-call(bf16[2,64,256]{2,1,0:T(8,128)(2,1)} %y_in.1, bf16[2,64,64]{2,1,0:T(8,128)(2,1)} %tri_in.1, bf16[64,64]{1,0:T(8,128)(2,1)} %coup_in.1, bf16[2560,2,1024]{2,1,0:T(2,128)(2,1)} %fac_ref.1, bf16[2560,256]{1,0:T(8,128)(2,1)} %rc_in.1, f32[1,256]{1,0:T(1,128)} %bitcast.1), custom_call_target="tpu_custom_call" | custom-call | tf_op jit(solution)/shard_map/pallas_call | solution.py:441
  67.5 1.5 %copy.10 = bf16[2,64,256]{2,1,0:T(8,128)(2,1)} copy(bf16[2,64,256]{2,1,0:T(8,128)(2,1)} %get-tuple-element.4) | data formatting | bytes 131072
  69.0 1.6 %copy.11 = bf16[160,512]{1,0:T(8,128)(2,1)} copy(bf16[160,512]{1,0:T(8,128)(2,1)} %get-tuple-element.5) | data formatting | bytes 327680

commit v3 on v2

--- a/solution.py
+++ b/solution.py
@@ -114,8 +114,8 @@
         rc_x.append(copy(view.at[:, lax.rem(x + d, SIDE), 0], rca.at[d], (r, xcol(d))))
         rc_y.append(copy(view.at[lax.rem(y + d, SIDE), :, 1], rcb.at[d], (r, ycol(d))))
 
-    for d in (2, 1, 3):
-        exchange(d)
+    exchange(1)
+    exchange(3)
 
     def product(k):
         p, q = CHUNKS[k]
@@ -157,10 +157,10 @@
     is0 = core == 0
 
     class Upper:
-        def __init__(self, cc, to, out, come):
+        def __init__(self, cc, to, out, come, sizes=range(SIDE)):
             k = count[0]
             count[0] += 1
-            self.out, self.come = out, come
+            self.out, self.come, self.sizes = out, come, sizes
             self.made = [
                 pltpu.make_async_remote_copy(
                     src_ref=tt.at[core, cc, pl.ds(0, 2 * v + 2)],
@@ -170,16 +170,16 @@
                 )
                 for v in range(SIDE)
             ]
-            for v in range(SIDE):
+            for v in sizes:
                 pl.when(out == v)(self.made[v].start)
             started.append(self)
 
         def wait_recv(self):
-            for v in range(SIDE):
+            for v in self.sizes:
                 pl.when(self.come == v)(self.made[v].wait_recv)
 
         def wait_send(self):
-            for v in range(SIDE):
+            for v in self.sizes:
                 pl.when(self.out == v)(self.made[v].wait_send)
 
     def whole(cc, to):
@@ -247,9 +247,14 @@
         for made in t_b[e, 1] + t_b[e, 3]:
             made.wait_recv()
         far = behind(e, 2)[1]
+        (low, low_size, _), (high, high_size, _) = behind(e, 1), behind(e, 3)
+        up, down = (r, slab(0, 1)), (r, slab(0, 3))
+        last = SIDE - 1
         t_far[e] = (
-            Upper(behind(e, 3)[0], (r, slab(0, 3)), behind(e, 3)[1], far),
-            whole(behind(e, 1)[0], (r, slab(0, 1))),
+            Upper(high, down, high_size, far, range(last)),
+            Upper(low, up, low_size, far, (last,)),
+            Maybe(cg.at[core, low], cg.at[core, low], up, low_size != last, far != last),
+            Maybe(cg.at[core, high], cg.at[core, high], down, high_size == last, far == last),
         )
         to_partner(e, 1)
         to_partner(e, 3)
@@ -327,6 +332,7 @@
     rhs1 = rhs(1).astype(BF16)
     for made in t_d:
         made.wait_recv()
+    exchange(2)
     second = jnp.concatenate([upper(1, rhs1, q) for q in range(4)], axis=1).astype(BF16)
     cross = jnp.concatenate(
         [
@@ -433,17 +439,29 @@
         made.wait_send()
 
 
+def settle(panel_in, dens_in, panel_out, dens_out, sem):
+    moves = [
+        pltpu.make_async_copy(panel_in, panel_out, sem.at[0]),
+        pltpu.make_async_copy(dens_in, dens_out, sem.at[1]),
+    ]
+    for move in moves:
+        move.start()
+    for move in moves:
+        move.wait()
+
+
 def body(y_panels, tri_inverse, coupling, rest_factor, rest_coeffs, occupations):
     rest = rest_coeffs.shape[0]
     vmem = pl.BlockSpec(memory_space=pltpu.VMEM)
     anywhere = pl.BlockSpec(memory_space=pltpu.HBM)
     copies = 300
-    return pl.pallas_call(
+    shapes = (
+        jax.ShapeDtypeStruct((2, 64, 256), BF16),
+        jax.ShapeDtypeStruct((160, 512), BF16),
+    )
+    results = pl.pallas_call(
         kernel,
-        out_shape=(
-            jax.ShapeDtypeStruct((2, 64, 256), BF16),
-            jax.ShapeDtypeStruct((160, 512), BF16),
-        ),
+        out_shape=shapes,
         in_specs=[anywhere] * 6,
         out_specs=(vmem, vmem),
         scratch_shapes=[
@@ -483,6 +501,14 @@
             collective_id=0, has_side_effects=True, vmem_limit_bytes=60 * 1024 * 1024
         ),
     )(y_panels, tri_inverse, coupling, rest_factor, rest_coeffs, occupations.reshape(1, 256))
+    return pl.pallas_call(
+        settle,
+        out_shape=shapes,
+        in_specs=[vmem, vmem],
+        out_specs=(anywhere, anywhere),
+        scratch_shapes=[pltpu.SemaphoreType.DMA((2,))],
+        compiler_params=pltpu.CompilerParams(vmem_limit_bytes=60 * 1024 * 1024),
+    )(*results)
 
 
 def solution(mesh):

time: 70.8 us -> 70 us (0.989)
  local copies, waits for them, and re-layouts: 3.07 us -> 0 us
  Pallas kernels: 66.9 us -> 69.2 us
    unnamed x2 -> x0, local copies, waits for them, and re-layouts: 3.07 us -> none
    pallas_call x1 -> x2, Pallas kernels: 66.9 us -> 69.2 us  [the longest x1 67.6 us: body(): pl.pallas_call(kernel, out_shape=shapes, in_specs=[anywhere] * 6, out_spe...]
where the time goes in v3:
time: 70 us; the launch traced here: 69.9 us
  Pallas kernels  69.2 us (99%)
    pallas_call x1, Pallas kernels, body(): pl.pallas_call(kernel, out_shape=shapes, in_specs=[anywhere] * 6, out_spe...  67.6 us
    pallas_call x1, Pallas kernels, body(): pl.pallas_call(settle, out_shape=shapes, in_specs=[vmem, vmem], out_specs...  1.66 us

profile of v3, /device:TPU:1, one launch (start us, length us, event | category | flops | bytes accessed | tf_op | source)
XLA Modules:
  0.0 69.9 jit_solution(335698204979872385)
XLA Ops:
  0.6 67.6 %shard_map.77 = (bf16[2,64,256]{2,1,0:T(8,128)(2,1)}, bf16[160,512]{1,0:T(8,128)(2,1)}) custom-call(bf16[2,64,256]{2,1,0:T(8,128)(2,1)} %y_in.1, bf16[2,64,64]{2,1,0:T(8,128)(2,1)} %tri_in.1, bf16[64,64]{1,0:T(8,128)(2,1)} %coup_in.1, bf16[2560,2,1024]{2,1,0:T(2,128)(2,1)} %fac_ref.1, bf16[2560,256]{1,0:T(8,128)(2,1)} %rc_in.1, f32[1,256]{1,0:T(1,128)} %bitcast.1), custom_call_target="tpu_custom_call" | custom-call | tf_op jit(solution)/shard_map/pallas_call | solution.py:462
  68.2 1.7 %shard_map.78 = (bf16[2,64,256]{2,1,0:T(8,128)(2,1)}, bf16[160,512]{1,0:T(8,128)(2,1)}) custom-call(bf16[2,64,256]{2,1,0:T(8,128)(2,1)} %get-tuple-element.4.panel_in, bf16[160,512]{1,0:T(8,128)(2,1)} %get-tuple-element.5.dens_in), custom_call_target="tpu_custom_call" | custom-call | tf_op jit(solution)/shard_map/pallas_call | solution.py:504

commit v4 on v3

--- a/solution.py
+++ b/solution.py
@@ -114,8 +114,8 @@
         rc_x.append(copy(view.at[:, lax.rem(x + d, SIDE), 0], rca.at[d], (r, xcol(d))))
         rc_y.append(copy(view.at[lax.rem(y + d, SIDE), :, 1], rcb.at[d], (r, ycol(d))))
 
-    exchange(1)
-    exchange(3)
+    for d in (2, 1, 3):
+        exchange(d)
 
     def product(k):
         p, q = CHUNKS[k]
@@ -332,7 +332,6 @@
     rhs1 = rhs(1).astype(BF16)
     for made in t_d:
         made.wait_recv()
-    exchange(2)
     second = jnp.concatenate([upper(1, rhs1, q) for q in range(4)], axis=1).astype(BF16)
     cross = jnp.concatenate(
         [
@@ -353,7 +352,7 @@
     sc[0, core, z] = (strip.astype(F32) * (weight * 0.015625)).astype(BF16)
 
     s_z, s_x, s_y = [], [], []
-    for d in (4, 3, 5, 2, 6, 1, 7):
+    for d in (1, 7, 4, 2, 6, 3, 5):
         s_z.append((d, copy(sc.at[0, core, z], sc.at[0, core, z], zdev(d))))
 
     def spread_out(zz, zin):
@@ -370,7 +369,7 @@
         po[zz, 1] = second[:, zz * 128:(zz + 1) * 128]
     pr[core, z] = po[z]
 
-    for d, made in s_z[::-1]:
+    for d, made in s_z[:2] + s_z[3:] + s_z[2:3]:
         made.wait_recv()
         zz = lax.rem(z + NZ - d, NZ)
         spread_out(zz, zz)

time: 70 us -> 67.7 us (0.967)
  Pallas kernels: 69.2 us -> 66.9 us
    pallas_call x1, Pallas kernels: 67.6 us -> 65.3 us  [body(): pl.pallas_call(kernel, out_shape=shapes, in_specs=[anywhere] * 6, out_spe...]
where the time goes in v4:
time: 67.7 us; the launch traced here: 67.6 us
  Pallas kernels  66.9 us (99%)
    pallas_call x1, Pallas kernels, body(): pl.pallas_call(kernel, out_shape=shapes, in_specs=[anywhere] * 6, out_spe...  65.3 us
    pallas_call x1, Pallas kernels, body(): pl.pallas_call(settle, out_shape=shapes, in_specs=[vmem, vmem], out_specs...  1.66 us

profile of v4, /device:TPU:1, one launch (start us, length us, event | category | flops | bytes accessed | tf_op | source)
XLA Modules:
  0.0 67.6 jit_solution(14342092926930145814)
XLA Ops:
  0.6 65.3 %shard_map.77 = (bf16[2,64,256]{2,1,0:T(8,128)(2,1)}, bf16[160,512]{1,0:T(8,128)(2,1)}) custom-call(bf16[2,64,256]{2,1,0:T(8,128)(2,1)} %y_in.1, bf16[2,64,64]{2,1,0:T(8,128)(2,1)} %tri_in.1, bf16[64,64]{1,0:T(8,128)(2,1)} %coup_in.1, bf16[2560,2,1024]{2,1,0:T(2,128)(2,1)} %fac_ref.1, bf16[2560,256]{1,0:T(8,128)(2,1)} %rc_in.1, f32[1,256]{1,0:T(1,128)} %bitcast.1), custom_call_target="tpu_custom_call" | custom-call | tf_op jit(solution)/shard_map/pallas_call | solution.py:461
  65.9 1.7 %shard_map.78 = (bf16[2,64,256]{2,1,0:T(8,128)(2,1)}, bf16[160,512]{1,0:T(8,128)(2,1)}) custom-call(bf16[2,64,256]{2,1,0:T(8,128)(2,1)} %get-tuple-element.4.panel_in, bf16[160,512]{1,0:T(8,128)(2,1)} %get-tuple-element.5.dens_in), custom_call_target="tpu_custom_call" | custom-call | tf_op jit(solution)/shard_map/pallas_call | solution.py:503

commit v5 on v4

--- a/solution.py
+++ b/solution.py
@@ -279,7 +279,6 @@
     zs.append(combine(1, pairs[1]))
     pairs.append(product(2))
     pairs.append(product(3))
-    to_axis_b(0)
     zs.append(combine(2, pairs[2]))
 
     for e in (1, 3, 2):
@@ -287,6 +286,7 @@
             made.wait_recv()
         to_axis_b(e)
         if e == 1:
+            to_axis_b(0)
             zs.append(combine(3, pairs[3]))
         if e == 3:
             onward(0)

time: 67.7 us -> 69.9 us (1.032)
  Pallas kernels: 66.9 us -> 69.2 us
    pallas_call x1, Pallas kernels: 65.3 us -> 67.5 us  [body(): pl.pallas_call(kernel, out_shape=shapes, in_specs=[anywhere] * 6, out_spe...]
where the time goes in v5:
time: 69.9 us; the launch traced here: 69.8 us
  Pallas kernels  69.2 us (99%)
    pallas_call x1, Pallas kernels, body(): pl.pallas_call(kernel, out_shape=shapes, in_specs=[anywhere] * 6, out_spe...  67.5 us
    pallas_call x1, Pallas kernels, body(): pl.pallas_call(settle, out_shape=shapes, in_specs=[vmem, vmem], out_specs...  1.66 us

profile of v5, /device:TPU:1, one launch (start us, length us, event | category | flops | bytes accessed | tf_op | source)
XLA Modules:
  0.0 69.8 jit_solution(17129175966488128597)
XLA Ops:
  0.6 67.5 %shard_map.77 = (bf16[2,64,256]{2,1,0:T(8,128)(2,1)}, bf16[160,512]{1,0:T(8,128)(2,1)}) custom-call(bf16[2,64,256]{2,1,0:T(8,128)(2,1)} %y_in.1, bf16[2,64,64]{2,1,0:T(8,128)(2,1)} %tri_in.1, bf16[64,64]{1,0:T(8,128)(2,1)} %coup_in.1, bf16[2560,2,1024]{2,1,0:T(2,128)(2,1)} %fac_ref.1, bf16[2560,256]{1,0:T(8,128)(2,1)} %rc_in.1, f32[1,256]{1,0:T(1,128)} %bitcast.1), custom_call_target="tpu_custom_call" | custom-call | tf_op jit(solution)/shard_map/pallas_call | solution.py:461
  68.2 1.7 %shard_map.78 = (bf16[2,64,256]{2,1,0:T(8,128)(2,1)}, bf16[160,512]{1,0:T(8,128)(2,1)}) custom-call(bf16[2,64,256]{2,1,0:T(8,128)(2,1)} %get-tuple-element.4.panel_in, bf16[160,512]{1,0:T(8,128)(2,1)} %get-tuple-element.5.dens_in), custom_call_target="tpu_custom_call" | custom-call | tf_op jit(solution)/shard_map/pallas_call | solution.py:503
